TPU v7x, 256 devices: a whole 4x4x8 slice. The times are simulated.
256 devices in a mesh: prow: 16 (over z, core), pcol: 16 (over x, y).
Axes of the slice: x: 4, y: 4, z: 8, core: 2. Of those that a mesh axis runs over, the one named last changes fastest.
Arguments:
- inv_lead: float32 [4, 16, 256, 4, 16, 256], P(None, 'prow', None, None, 'pcol'), may hold values from -1 to 2, as said below
- h_lead: float32 [4, 16, 256, 6, 16, 256], P(None, 'pcol', None, None, 'prow'), may hold values from -6 to 6
- h_slab: float32 [512, 6, 16, 256], P('pcol', None, 'prow'), may hold values from -6 to 6
- l_panel: float32 [512, 4, 16, 256], P('pcol', None, 'prow'), may hold values from -0.046875 to 0.046875
- l_diag: float32 [512, 512], replicated, may hold values from -1 to 2, as said below
Outputs:
- x_slab: float32 [512, 6, 16, 256], P('pcol', None, 'prow')
- y_lead: float32 [512, 4, 16, 256], P('pcol', None, 'prow')
- y_diag: float32 [512, 512], P('pcol', 'prow')
Inputs may be any that keep to these rules, and one draw needn't show every extreme that they name: inv_lead is lower triangular in natural order, with diagonal entries between 1 and 2. l_diag is lower triangular, with diagonal entries between 1 and 2.
All inputs are finite; a program needn't handle non-finite values.
Results may differ from a plain program's by a relative error of at most 0.00018.
Values sent between devices are 32-bit elements; how exact they have to be, the bound alone decides.
No kernel may reach another device: no remote copies, remote signals or barrier semaphores. Data moves between devices by JAX's collectives and lax.ppermute only.
A program may use at most 128 MiB of HBM per device.

v0:
```python
import jax
import jax.numpy as jnp
from jax import lax
from jax.sharding import PartitionSpec as P


def copy_for_each(value, axis):
    copies = jnp.broadcast_to(value, (lax.axis_size(axis), *value.shape))
    return lax.all_to_all(copies, axis, split_axis=0, concat_axis=0, tiled=True)


def joined_along(parts, dim):
    lengths = list(parts.shape[1:])
    lengths[dim] *= parts.shape[0]
    return jnp.moveaxis(parts, 0, dim).reshape(lengths)


def gathered_copies(value, axis, dim):
    parts = copy_for_each(value, axis)
    return joined_along(parts, dim)


def in_blocks(value, dim, size):
    lengths = value.shape
    parts = value.reshape(*lengths[:dim], size, lengths[dim] // size, *lengths[dim + 1 :])
    return jnp.moveaxis(parts, dim, 0)


def sum_at_owner(value, axis, dim):
    parts = in_blocks(value, dim, lax.axis_size(axis))
    arrived = lax.all_to_all(parts, axis, split_axis=0, concat_axis=0, tiled=True)
    return arrived.sum(axis=0)


def in_one_piece(arrays, axis, dim, along):
    widths = [a.shape[along] for a in arrays]
    both = jnp.concatenate(arrays, axis=along)
    result = lax.psum_scatter(both, axis, scatter_dimension=dim, tiled=True)
    return tuple(jnp.split(result, [sum(widths[:k]) for k in range(1, len(widths))], axis=along))


def matmul_hi(left, right):
    return jnp.dot(left, right, precision=lax.Precision.HIGHEST, preferred_element_type=jnp.float32)


def matmul_trans(left, right):
    return lax.dot_general(
        left,
        right,
        (((1,), (1,)), ((), ())),
        precision=lax.Precision.HIGHEST,
        preferred_element_type=jnp.float32,
    )


def invert_diag(l_diag, block_size):
    diag_top = l_diag[:block_size, :block_size]
    diag_bottom = l_diag[block_size:, block_size:]
    off_block = l_diag[block_size:, :block_size]
    identity = jnp.eye(block_size, dtype=jnp.float32)
    top_inv = lax.linalg.triangular_solve(diag_top, identity, left_side=True, lower=True)
    bottom_inv = lax.linalg.triangular_solve(diag_bottom, identity, left_side=True, lower=True)
    corner = -matmul_hi(bottom_inv, matmul_hi(off_block, top_inv))
    upper_rows = jnp.concatenate([top_inv, jnp.zeros_like(top_inv)], axis=1)
    lower_rows = jnp.concatenate([corner, bottom_inv], axis=1)
    return jnp.concatenate([upper_rows, lower_rows], axis=0)


def per_device(inv_lead, h_lead, h_slab, l_panel, l_diag):
    slab_rows = l_diag.shape[0]
    block_size = l_panel.shape[3]
    prev_blocks = l_panel.shape[1]
    x_rows = l_panel.shape[0]
    h_blocks = h_slab.shape[1]
    diag_inv = invert_diag(l_diag, slab_rows // 2)
    inv_local = inv_lead.reshape(prev_blocks * block_size, -1)
    col_width = inv_local.shape[1]
    col_blocks = col_width // block_size
    h_local = h_lead.reshape(col_width, -1)
    h_side = h_slab.reshape(x_rows, -1)
    y_rows = slab_rows // lax.axis_size("prow")
    row_start = lax.axis_index("prow") * y_rows
    col_start = lax.axis_index("pcol") * x_rows
    piece = gathered_copies(l_panel, "pcol", 0)
    factor = matmul_hi(diag_inv, piece.reshape(piece.shape[0], -1))
    side_term = matmul_hi(lax.dynamic_slice_in_dim(diag_inv, col_start, x_rows, 1), h_side)
    own_panel = sum_at_owner(-matmul_hi(factor, inv_local), "prow", 0)
    product = matmul_hi(lax.all_gather(own_panel, "prow", axis=0, tiled=True), h_local)
    x_local = sum_at_owner(product + side_term, "pcol", 0)
    x_slab = x_local.reshape(x_rows, h_blocks, 1, block_size)
    kept_cols = x_slab[:, : prev_blocks + 1]
    widened = lax.all_gather(kept_cols, "prow", axis=2, tiled=True).reshape(x_rows, -1)
    prev_rows = prev_blocks * block_size * lax.axis_size("prow")
    head_cols = widened[:, :prev_rows]
    tail_cols = widened[:, prev_rows : prev_rows + slab_rows]
    shifted_x = lax.all_to_all(
        head_cols.reshape(x_rows, col_blocks, lax.axis_size("pcol"), block_size),
        "pcol",
        split_axis=2,
        concat_axis=0,
        tiled=True,
    )
    shifted_x = shifted_x.reshape(slab_rows, col_width)
    lead_part = matmul_trans(shifted_x, inv_local)
    diag_part = matmul_trans(shifted_x, own_panel)
    y_first, y_block = in_one_piece((lead_part, diag_part), "pcol", 0, 1)
    diag_rows = lax.dynamic_slice_in_dim(diag_inv, row_start, y_rows, 0)
    y_diag = y_block + matmul_trans(tail_cols, diag_rows)
    return (x_slab, y_first.reshape(x_rows, prev_blocks, 1, block_size), y_diag)


def solution(mesh):
    return jax.shard_map(
        per_device,
        mesh=mesh,
        in_specs=(
            P(None, "prow", None, None, "pcol", None),
            P(None, "pcol", None, None, "prow", None),
            P("pcol", None, "prow", None),
            P("pcol", None, "prow", None),
            P(),
        ),
        out_specs=(P("pcol", None, "prow", None), P("pcol", None, "prow", None), P("pcol", "prow")),
        check_vma=False,
    )
```

profile of v0, /device:TPU:2, one launch (start us, length us, event | category | flops | bytes accessed | tf_op | source)
XLA Modules:
  0.0 457.1 jit_solution(1383191247335577584)
XLA Ops:
  8.1 2.9 broadcast_in_dim.4
  11.1 7.5 %all-to-all-start = ((f32[16,32,4,1,256]{4,3,2,1,0:T(1,128)}), f32[16,32,4,1,256]{4,3,2,1,0:T(1,128)S(1)}, u32[]{:S(2)}, u32[]{:S(2)}) async-start(f32[16,32,4,1,256]{4,3,2,1,0:T(1,128)} %broadcast_in_dim.4), calls=%async_computation | async-start | bytes 4194304 | tf_op jit(solution)/shard_map/all_to_all | solution.py:9
  19.8 3.8 while.4
  23.6 19.7 %custom-call.4 = f32[2,128,128]{1,2,0:T(8,128)S(1)} custom-call(f32[2,128,128]{2,1,0:T(8,128)S(1)} %get-tuple-element.18), custom_call_target="InvertDiagBlocksLowerTriangular" | custom-call | tf_op jit(solution)/shard_map/triangular_solve/custom-call.1 | solution.py:61
  43.3 4.0 while.5
  43.9 1.4 bitcast_dynamic-update-slice_fusion.5
  45.9 1.4 bitcast_dynamic-update-slice_fusion.5
  47.3 19.7 %custom-call.5 = f32[2,128,128]{1,2,0:T(8,128)S(1)} custom-call(f32[2,128,128]{2,1,0:T(8,128)S(1)} %get-tuple-element.19), custom_call_target="InvertDiagBlocksLowerTriangular" | custom-call | tf_op jit(solution)/shard_map/triangular_solve/custom-call.1 | solution.py:62
  67.0 14.2 %reduce.1 = f32[4,256,4,256]{3,2,1,0:T(4,128)} reduce(f32[4,1,256,4,1,256]{5,4,3,2,1,0:T(1,128)} %param.7, f32[]{:T(128)} %constant.47), dimensions={1,4}, to_apply=%param.7.reduce_sub_computation | reduce | bytes 8388612 | tf_op args[0]
  81.2 5.2 %copy.34 = f32[128,8,4,256]{3,1,2,0:T(8,128)} copy(f32[128,8,4,256]{3,2,1,0:T(4,128)} %bitcast.82) | data formatting | bytes 8388608
  88.2 1.5 fusion.6
  90.2 7.4 %reduce = f32[16,32,4,256]{3,2,1,0:T(4,128)} reduce(f32[16,32,4,1,256]{4,3,2,1,0:T(1,128)S(1)} %all-to-all-done, f32[]{:T(128)} %constant.47), dimensions={3}, to_apply=%all_to_all.20.reduce_sub_computation | reduce | bytes 4194308 | tf_op jit(solution)/shard_map/all_to_all | solution.py:9
  97.6 2.1 copy.33
  99.7 4.0 fusion.22
  103.7 6.9 %convolution_negate_fusion = f32[512,1024]{1,0:T(8,128)S(1)} fusion(f32[512,1024]{1,0:T(8,128)S(1)} %fusion.22, f32[1024,1024]{1,0:T(8,128)S(1)} %bitcast.77), kind=kOutput, calls=%fused_computation.6 | convolution fusion | flops 6442975232 | bytes 8388608 | tf_op jit(solution)/shard_map/dot_general | solution.py:43
  110.6 58.0 %all_to_all.31 = f32[16,32,1024]{2,1,0:T(8,128)S(1)} all-to-all(f32[16,32,1024]{2,1,0:T(8,128)S(1)} %bitcast.92), channel_id=1, replica_groups=mesh['prow'=16,'pcol'=16] {'prow'}, dimensions={0} | all-to-all | bytes 4194304 | tf_op jit(solution)/shard_map/all_to_all | solution.py:31
  169.5 37.4 %reduce.2 = f32[4,256,6,256]{3,2,1,0:T(8,128)} reduce(f32[4,1,256,6,1,256]{5,4,3,2,1,0:T(1,128)} %param.8, f32[]{:T(128)} %constant.47), dimensions={1,4}, to_apply=%param.8.reduce_sub_computation | reduce | bytes 12582916 | tf_op args[1]
  206.8 9.2 %copy.35 = f32[128,8,6,256]{3,1,2,0:T(8,128)} copy(f32[128,8,6,256]{3,2,1,0:T(8,128)} %bitcast.79) | data formatting | bytes 12582912
  216.8 13.7 %fusion.25 = f32[512,1536]{1,0:T(8,128)S(1)} fusion(f32[512,1024]{1,0:T(8,128)} %all-gather.3.cloned.1.call-done, f32[1024,1536]{1,0:T(8,128)} %bitcast.93), kind=kOutput, calls=%fused_computation.47 | convolution fusion | flops 9663676416 | bytes 11534336 | tf_op jit(solution)/shard_map/dot_general | solution.py:43
  230.4 2.8 convolution_add_fusion
  233.2 45.1 %all_to_all.32 = f32[16,32,1536]{2,1,0:T(8,128)S(1)} all-to-all(f32[16,32,1536]{2,1,0:T(8,128)S(1)} %bitcast.83), channel_id=1, replica_groups=mesh['prow'=16,'pcol'=16] {'pcol'}, dimensions={0} | all-to-all | bytes 6291456 | tf_op jit(solution)/shard_map/all_to_all | solution.py:31
  279.4 36.6 %all-gather.5.cloned.1.call-done = f32[32,5,16,256]{3,0,1,2:T(8,128)} async-done(((f32[32,5,1,256]{3,0,1,2:T(8,128)}), f32[32,5,16,256]{3,0,1,2:T(8,128)}) %all-gather.5.cloned.1.call-update) | async-done | bytes 2621456 | tf_op jit(solution)/shard_map/all_gather | solution.py:92
  315.9 3.3 copy.25
  319.2 1.5 copy.37
  321.5 1.4 copy.26
  322.9 33.8 %all_to_all.30 = f32[32,4,16,256]{3,1,0,2:T(4,128)S(1)} all-to-all(f32[32,4,16,256]{3,1,0,2:T(4,128)S(1)} %copy.26), channel_id=1, replica_groups=mesh['prow'=16,'pcol'=16] {'pcol'}, dimensions={2} | all-to-all | bytes 4194304 | tf_op jit(solution)/shard_map/all_to_all | solution.py:96
  357.1 1.7 copy-done.1
  358.8 7.0 %fusion.26 = f32[512,1024]{1,0:T(8,128)S(1)} fusion(f32[512,1024]{1,0:T(8,128)S(1)} %bitcast.80, f32[1024,1024]{1,0:T(8,128)S(1)} %bitcast.78), kind=kOutput, calls=%fused_computation.48 | convolution fusion | flops 6442450944 | bytes 8388608 | tf_op jit(solution)/shard_map/dot_general | solution.py:47
  365.8 1.8 fusion.27
  367.6 1.6 pad_maximum_fusion
  370.1 76.6 %reduce-scatter.2.cloned.1.call-done = f32[32,1056]{1,0:T(8,128)} async-done(((f32[512,1056]{1,0:T(8,128)}), f32[32,1056]{1,0:T(8,128)}) %reduce-scatter.2.cloned.1.call-update) | async-done | bytes 135184 | tf_op jit(solution)/shard_map/reduce_scatter | solution.py:38
  448.5 1.6 convolution_add_fusion.1
  (55 shorter events, 15.7 us)
Async XLA Ops:
  11.1 79.2 %all-to-all-start = ((f32[16,32,4,1,256]{4,3,2,1,0:T(1,128)}), f32[16,32,4,1,256]{4,3,2,1,0:T(1,128)S(1)}, u32[]{:S(2)}, u32[]{:S(2)}) async-start(f32[16,32,4,1,256]{4,3,2,1,0:T(1,128)} %broadcast_in_dim.4), calls=%async_computation | async-start | bytes 4194304 | tf_op jit(solution)/shard_map/all_to_all | solution.py:9
  18.5 198.2 %all-gather.3.cloned.1.call-start = ((), (), s32[]{:S(2)}) async-start(), calls=%async_computation.5 | async-start | bytes 2228224 | tf_op jit(solution)/shard_map/all_gather | solution.py:88
  99.7 4.0 copy-start
  169.4 146.5 %all-gather.5.cloned.1.call-start = ((), (), s32[]{:S(2)}) async-start(), calls=%async_computation.6 | async-start | bytes 2785280 | tf_op jit(solution)/shard_map/all_gather | solution.py:92
  206.8 9.2 %copy-start.4 = (f32[32,6,1,256]{3,2,1,0:T(1,128)S(1)}, f32[32,6,1,256]{3,2,1,0:T(1,128)}, u32[]{:S(2)}) copy-start(f32[32,6,1,256]{3,2,1,0:T(1,128)} %param.9) | copy-start | bytes 589828
  216.7 13.7 %copy-start.2 = (f32[512,512]{1,0:T(8,128)}, f32[512,512]{1,0:T(8,128)S(1)}, u32[]{:S(2)}) copy-start(f32[512,512]{1,0:T(8,128)S(1)} %select_maximum_fusion) | copy-start | bytes 3145732
  279.3 167.4 %reduce-scatter.2.cloned.1.call-start = ((), (), s32[]{:S(2)}) async-start(), calls=%async_computation.7 | async-start | bytes 2506752 | tf_op jit(solution)/shard_map/reduce_scatter | solution.py:38
  356.7 2.2 copy-start.1
  358.8 7.0 %copy-start.3 = (f32[32,1024]{1,0:T(8,128)S(1)}, f32[32,1024]{1,0:T(8,128)}, u32[]{:S(2)}) copy-start(f32[32,1024]{1,0:T(8,128)} %reduce_sum.18) | copy-start | bytes 393220
Sparse Core Ops, SparseCore 0:
  169.5 37.7 all-gather.2
  279.4 36.4 all-gather.4
  369.4 77.3 reduce-scatter.1
where the time goes:
time: 464 us; the launch traced here: 457 us
  blocking collectives  137 us (30%)
  waiting for transfers between devices  113 us (24%)
  other arithmetic  103 us (22%)
  matrix products  41.4 us (9%)
  local copies, waits for them, and re-layouts  40.7 us (9%)
  between operations  14.5 us (3%)
  starting transfers between devices  7.6 us (2%)
    all_to_all x2, blocking collectives, sum_at_owner(): lax.all_to_all(parts, axis, split_axis=0, concat_axis=0, tiled=True)  103 us
    reduce_scatter x1, waiting for transfers between devices, in_one_piece(): result = lax.psum_scatter(both, axis, scatter_dimension=dim, tiled=True)  76.6 us
    unnamed x3, other arithmetic  52.1 us
    all_gather x1, waiting for transfers between devices, per_device(): lax.all_gather(kept_cols, 'prow', axis=2, tiled=True).reshape(x_rows, -1)  36.6 us
    all_to_all x1, blocking collectives, per_device(): lax.all_to_all(head_cols.reshape(x_rows, col_blocks, lax.axis_size('pcol'...  33.8 us
    dot_general x6, matrix products, matmul_hi(): jnp.dot(left, right, precision=lax.Precision.HIGHEST, preferred_element_t...  29.3 us
    unnamed x19, local copies, waits for them, and re-layouts  22.7 us
    another operation x2, other arithmetic, invert_diag(): lax.linalg.triangular_solve(diag_bottom, identity, left_side=True, lower=...  20.7 us
  transfers between devices with their start and end apart: 4, of which 2 were waited for; matrix products, arithmetic and copies ran while one was open for 26% of the time, Pallas kernels for 0%

commit v1 on v0

--- a/solution.py
+++ b/solution.py
@@ -89,7 +89,10 @@
     x_local = sum_at_owner(product + side_term, "pcol", 0)
     x_slab = x_local.reshape(x_rows, h_blocks, 1, block_size)
     kept_cols = x_slab[:, : prev_blocks + 1]
-    widened = lax.all_gather(kept_cols, "prow", axis=2, tiled=True).reshape(x_rows, -1)
+    keep_up_the_trails = lambda load: jnp.concatenate(
+        lax.all_gather(load, axis_name="prow"), axis=2
+    )
+    widened = keep_up_the_trails(kept_cols).reshape(x_rows, -1)
     prev_rows = prev_blocks * block_size * lax.axis_size("prow")
     head_cols = widened[:, :prev_rows]
     tail_cols = widened[:, prev_rows : prev_rows + slab_rows]

time: 464 us -> 466 us (level)
    unnamed x19 -> x21, local copies, waits for them, and re-layouts: 22.7 us -> 20.3 us
where the time goes in v1:
time: 466 us; the launch traced here: 459 us
  blocking collectives  137 us (29%)
  waiting for transfers between devices  114 us (24%)
  other arithmetic  103 us (22%)
  local copies, waits for them, and re-layouts  41.8 us (9%)
  matrix products  41.4 us (9%)
  between operations  14.5 us (3%)
  starting transfers between devices  7.6 us (2%)
    all_to_all x2, blocking collectives, sum_at_owner(): lax.all_to_all(parts, axis, split_axis=0, concat_axis=0, tiled=True)  103 us
    reduce_scatter x1, waiting for transfers between devices, in_one_piece(): result = lax.psum_scatter(both, axis, scatter_dimension=dim, tiled=True)  77.5 us
    unnamed x3, other arithmetic  52.1 us
    all_gather x1, waiting for transfers between devices, per_device(): lax.all_gather(load, axis_name='prow')  36.6 us
    all_to_all x1, blocking collectives, per_device(): lax.all_to_all(head_cols.reshape(x_rows, col_blocks, lax.axis_size('pcol'...  33.8 us
    dot_general x6, matrix products, matmul_hi(): jnp.dot(left, right, precision=lax.Precision.HIGHEST, preferred_element_t...  29.3 us
    another operation x2, other arithmetic, invert_diag(): lax.linalg.triangular_solve(diag_bottom, identity, left_side=True, lower=...  20.7 us
    unnamed x21, local copies, waits for them, and re-layouts  20.3 us
  transfers between devices with their start and end apart: 4, of which 2 were waited for; matrix products, arithmetic and copies ran while one was open for 26% of the time, Pallas kernels for 0%

profile of v1, /device:TPU:2, one launch (start us, length us, event | category | flops | bytes accessed | tf_op | source)
XLA Modules:
  0.0 459.0 jit_solution(12524832312606488522)
XLA Ops:
  8.1 2.9 broadcast_in_dim.4
  11.0 7.5 %all-to-all-start = ((f32[16,32,4,1,256]{4,3,2,1,0:T(1,128)}), f32[16,32,4,1,256]{4,3,2,1,0:T(1,128)S(1)}, u32[]{:S(2)}, u32[]{:S(2)}) async-start(f32[16,32,4,1,256]{4,3,2,1,0:T(1,128)} %broadcast_in_dim.4), calls=%async_computation | async-start | bytes 4194304 | tf_op jit(solution)/shard_map/all_to_all | solution.py:9
  19.8 3.9 while.4
  23.7 19.7 %custom-call.4 = f32[2,128,128]{1,2,0:T(8,128)S(1)} custom-call(f32[2,128,128]{2,1,0:T(8,128)S(1)} %get-tuple-element.18), custom_call_target="InvertDiagBlocksLowerTriangular" | custom-call | tf_op jit(solution)/shard_map/triangular_solve/custom-call.1 | solution.py:61
  43.4 4.0 while.5
  44.0 1.4 bitcast_dynamic-update-slice_fusion.5
  46.0 1.4 bitcast_dynamic-update-slice_fusion.5
  47.4 19.7 %custom-call.5 = f32[2,128,128]{1,2,0:T(8,128)S(1)} custom-call(f32[2,128,128]{2,1,0:T(8,128)S(1)} %get-tuple-element.19), custom_call_target="InvertDiagBlocksLowerTriangular" | custom-call | tf_op jit(solution)/shard_map/triangular_solve/custom-call.1 | solution.py:62
  67.1 14.2 %reduce.1 = f32[4,256,4,256]{3,2,1,0:T(4,128)} reduce(f32[4,1,256,4,1,256]{5,4,3,2,1,0:T(1,128)} %param.7, f32[]{:T(128)} %constant.47), dimensions={1,4}, to_apply=%param.7.reduce_sub_computation | reduce | bytes 8388612 | tf_op args[0]
  81.4 5.1 %copy.25 = f32[128,8,4,256]{3,1,2,0:T(8,128)} copy(f32[128,8,4,256]{3,2,1,0:T(4,128)} %bitcast.86) | data formatting | bytes 8388608
  88.3 1.5 fusion.6
  90.3 7.4 %reduce = f32[16,32,4,256]{3,2,1,0:T(4,128)} reduce(f32[16,32,4,1,256]{4,3,2,1,0:T(1,128)S(1)} %all-to-all-done, f32[]{:T(128)} %constant.47), dimensions={3}, to_apply=%all_to_all.20.reduce_sub_computation | reduce | bytes 4194308 | tf_op jit(solution)/shard_map/all_to_all | solution.py:9
  97.7 2.1 copy.24
  99.8 4.0 fusion.22
  103.7 6.9 %convolution_negate_fusion = f32[512,1024]{1,0:T(8,128)S(1)} fusion(f32[512,1024]{1,0:T(8,128)S(1)} %fusion.22, f32[1024,1024]{1,0:T(8,128)S(1)} %bitcast.81), kind=kOutput, calls=%fused_computation.7 | convolution fusion | flops 6442975232 | bytes 8388608 | tf_op jit(solution)/shard_map/dot_general | solution.py:43
  110.7 58.0 %all_to_all.31 = f32[16,32,1024]{2,1,0:T(8,128)S(1)} all-to-all(f32[16,32,1024]{2,1,0:T(8,128)S(1)} %bitcast.94), channel_id=1, replica_groups=mesh['prow'=16,'pcol'=16] {'prow'}, dimensions={0} | all-to-all | bytes 4194304 | tf_op jit(solution)/shard_map/all_to_all | solution.py:31
  169.5 37.4 %reduce.2 = f32[4,256,6,256]{3,2,1,0:T(8,128)} reduce(f32[4,1,256,6,1,256]{5,4,3,2,1,0:T(1,128)} %param.8, f32[]{:T(128)} %constant.47), dimensions={1,4}, to_apply=%param.8.reduce_sub_computation | reduce | bytes 12582916 | tf_op args[1]
  206.9 9.2 %copy.26 = f32[128,8,6,256]{3,1,2,0:T(8,128)} copy(f32[128,8,6,256]{3,2,1,0:T(8,128)} %bitcast.83) | data formatting | bytes 12582912
  216.8 13.7 %fusion.25 = f32[512,1536]{1,0:T(8,128)S(1)} fusion(f32[512,1024]{1,0:T(8,128)} %all-gather.4.cloned.1.call-done, f32[1024,1536]{1,0:T(8,128)} %bitcast.95), kind=kOutput, calls=%fused_computation.48 | convolution fusion | flops 9663676416 | bytes 11534336 | tf_op jit(solution)/shard_map/dot_general | solution.py:43
  230.5 2.8 convolution_add_fusion
  233.3 45.1 %all_to_all.32 = f32[16,32,1536]{2,1,0:T(8,128)S(1)} all-to-all(f32[16,32,1536]{2,1,0:T(8,128)S(1)} %bitcast.87), channel_id=1, replica_groups=mesh['prow'=16,'pcol'=16] {'pcol'}, dimensions={0} | all-to-all | bytes 6291456 | tf_op jit(solution)/shard_map/all_to_all | solution.py:31
  279.6 36.6 %all-gather.6.cloned.1.call-done = f32[512,5,1,256]{3,2,1,0:T(1,128)} async-done(((f32[32,5,1,256]{3,2,1,0:T(1,128)}), f32[512,5,1,256]{3,2,1,0:T(1,128)}) %all-gather.6.cloned.1.call-update) | async-done | bytes 2621456 | tf_op jit(solution)/shard_map/all_gather | solution.py:93
  316.2 3.3 copy.32
  319.5 1.8 reshape_reshape.7
  321.2 1.6 slice-done
  324.8 33.8 %all_to_all.30 = f32[32,4,16,256]{3,1,0,2:T(4,128)S(1)} all-to-all(f32[32,4,16,256]{3,1,0,2:T(4,128)S(1)} %copy.18), channel_id=1, replica_groups=mesh['prow'=16,'pcol'=16] {'pcol'}, dimensions={2} | all-to-all | bytes 4194304 | tf_op jit(solution)/shard_map/all_to_all | solution.py:99
  359.1 1.7 copy-done.1
  360.8 7.0 %fusion.26 = f32[512,1024]{1,0:T(8,128)S(1)} fusion(f32[512,1024]{1,0:T(8,128)S(1)} %bitcast.84, f32[1024,1024]{1,0:T(8,128)S(1)} %bitcast.82), kind=kOutput, calls=%fused_computation.49 | convolution fusion | flops 6442450944 | bytes 8388608 | tf_op jit(solution)/shard_map/dot_general | solution.py:47
  367.8 1.8 fusion.27
  369.6 1.6 pad_maximum_fusion
  371.2 77.5 %reduce-scatter.2.cloned.1.call-done = f32[32,1056]{1,0:T(8,128)} async-done(((f32[512,1056]{1,0:T(8,128)}), f32[32,1056]{1,0:T(8,128)}) %reduce-scatter.2.cloned.1.call-update) | async-done | bytes 135184 | tf_op jit(solution)/shard_map/reduce_scatter | solution.py:38
  450.4 1.6 convolution_add_fusion.1
  (59 shorter events, 16.3 us)
Async XLA Ops:
  11.0 79.3 %all-to-all-start = ((f32[16,32,4,1,256]{4,3,2,1,0:T(1,128)}), f32[16,32,4,1,256]{4,3,2,1,0:T(1,128)S(1)}, u32[]{:S(2)}, u32[]{:S(2)}) async-start(f32[16,32,4,1,256]{4,3,2,1,0:T(1,128)} %broadcast_in_dim.4), calls=%async_computation | async-start | bytes 4194304 | tf_op jit(solution)/shard_map/all_to_all | solution.py:9
  18.5 198.3 %all-gather.4.cloned.1.call-start = ((), (), s32[]{:S(2)}) async-start(), calls=%async_computation.5 | async-start | bytes 2228224 | tf_op jit(solution)/shard_map/all_gather | solution.py:88
  99.8 4.0 copy-start
  169.5 146.7 %all-gather.6.cloned.1.call-start = ((), (), s32[]{:S(2)}) async-start(), calls=%async_computation.7 | async-start | bytes 2785280 | tf_op jit(solution)/shard_map/all_gather | solution.py:93
  206.9 9.2 %copy-start.6 = (f32[32,6,1,256]{3,2,1,0:T(1,128)S(1)}, f32[32,6,1,256]{3,2,1,0:T(1,128)}, u32[]{:S(2)}) copy-start(f32[32,6,1,256]{3,2,1,0:T(1,128)} %param.9) | copy-start | bytes 589828
  216.8 13.7 %copy-start.3 = (f32[512,512]{1,0:T(8,128)}, f32[512,512]{1,0:T(8,128)S(1)}, u32[]{:S(2)}) copy-start(f32[512,512]{1,0:T(8,128)S(1)} %select_maximum_fusion) | copy-start | bytes 3145732
  278.8 40.7 %copy-start.5 = (f32[32,6,1,256]{3,2,1,0:T(1,128)}, f32[32,6,1,256]{3,2,1,0:T(1,128)S(1)}, u32[]{:S(2)}) copy-start(f32[32,6,1,256]{3,2,1,0:T(1,128)S(1)} %reshape.49) | copy-start | bytes 589828
  279.6 169.1 %reduce-scatter.2.cloned.1.call-start = ((), (), s32[]{:S(2)}) async-start(), calls=%async_computation.6 | async-start | bytes 2506752 | tf_op jit(solution)/shard_map/reduce_scatter | solution.py:38
  321.2 1.6 slice-start
  358.6 2.2 copy-start.1
  360.8 7.0 %copy-start.4 = (f32[32,1024]{1,0:T(8,128)S(1)}, f32[32,1024]{1,0:T(8,128)}, u32[]{:S(2)}) copy-start(f32[32,1024]{1,0:T(8,128)} %reduce_sum.18) | copy-start | bytes 393220
  371.2 79.2 %copy-start.2 = (f32[32,20480]{1,0:T(8,128)S(1)}, f32[32,20480]{1,0:T(8,128)}, u32[]{:S(2)}) copy-start(f32[32,20480]{1,0:T(8,128)} %reshape_reshape.7) | copy-start | bytes 7864324
Sparse Core Ops, SparseCore 0:
  169.6 37.7 all-gather.3
  279.7 36.4 all-gather.5
  371.3 77.3 reduce-scatter.1
